TPU v7x, 32 devices: a whole 2x2x4 slice. The times are simulated.
32 devices in a mesh: dp: 8 (over y, x, core), tensor: 4 (over z).
Axes of the slice: x: 2, y: 2, z: 4, core: 2. Of those that a mesh axis runs over, the one named last changes fastest.
Arguments:
- tokens: bfloat16 [8192, 1536], P(('dp', 'tensor')), may hold values from -6 to 6
- segments: int32 [8, 1024], P('dp'), may hold values from 0 to 3, never falling along the last dimension, each value on 1 to 512 neighbouring positions
- gain_one: bfloat16 [1536], P('dp'), may hold values from 0.25 to 1.75
- query_w: bfloat16 [1536, 1536], P('dp', 'tensor'), may hold values from -0.15625 to 0.15625
- query_b: bfloat16 [1536], P('tensor'), may hold values from -3 to 3
- key_w: bfloat16 [1536, 256], P('dp'), may hold values from -0.15625 to 0.15625
- key_b: bfloat16 [256], replicated, may hold values from -3 to 3
- value_w: bfloat16 [1536, 256], P('dp'), may hold values from -0.15625 to 0.15625
- value_b: bfloat16 [256], replicated, may hold values from -3 to 3
- out_w: bfloat16 [1536, 1536], P('dp', 'tensor'), may hold values from -0.4375 to 0.4375
- gain_two: bfloat16 [1536], P('dp'), may hold values from 0.25 to 1.75
- gate_w: bfloat16 [1536, 8960], P('dp', 'tensor'), may hold values from -0.15625 to 0.15625
- up_w: bfloat16 [1536, 8960], P('dp', 'tensor'), may hold values from -0.15625 to 0.15625
- down_w: bfloat16 [1536, 8960], P('dp', 'tensor'), may hold values from -0.0625 to 0.0625
- cotangent: bfloat16 [8192, 1536], P(('dp', 'tensor')), may hold values from -6 to 6
Outputs:
- mixed: bfloat16 [8192, 1536], P(('dp', 'tensor'))
- input_grad: bfloat16 [8192, 1536], P(('dp', 'tensor'))
- grad_gain_one: float32 [1536], P(('dp', 'tensor'))
- grad_query_w: float32 [1536, 1536], P('dp', 'tensor')
- grad_query_b: float32 [1536], P(('dp', 'tensor'))
- grad_key_w: float32 [1536, 256], P(('dp', 'tensor'))
- grad_key_b: float32 [256], replicated
- grad_value_w: float32 [1536, 256], P(('dp', 'tensor'))
- grad_value_b: float32 [256], replicated
- grad_out_w: float32 [1536, 1536], P('dp', 'tensor')
- grad_gain_two: float32 [1536], P(('dp', 'tensor'))
- grad_gate_w: float32 [1536, 8960], P('dp', 'tensor')
- grad_up_w: float32 [1536, 8960], P('dp', 'tensor')
- grad_down_w: float32 [1536, 8960], P('dp', 'tensor')
Inputs may be any that keep to these rules, and one draw needn't show every extreme that they name: `segments`: in each sequence of 1024 positions the document numbers never fall; each of the 4 documents covers 1 to 512 positions, and one covers exactly 512.
All inputs are finite; a program needn't handle non-finite values.
Results may differ from a plain program's by a relative error of at most 0.02.
Values may be sent and summed in bfloat16 or wider, within the bound.
A program may use at most 256 MiB of HBM per device.

v0:
```python
import jax
import jax.numpy as jnp
from jax import lax
from jax.sharding import PartitionSpec as P

KV_HEADS = 2
HEAD_DIM = 128
DOC_MAX = 512
EPSILON = 1e-06
ROPE_BASE = 1000000.0
NEGATIVE = -1e30


def angle_tables(first, length, head_width):
    position = (first + jnp.arange(length)).astype(jnp.float32)
    exponent = jnp.arange(head_width // 2, dtype=jnp.float32) * (2.0 / head_width)
    frequency = ROPE_BASE ** (-exponent)
    angle = position[:, None] * frequency[None, :]
    return (jnp.cos(angle), jnp.sin(angle))


def rotate(values, cosine, sine):
    half_width = values.shape[-1] // 2
    first_half = values[..., :half_width]
    second_half = values[..., half_width:]
    return jnp.concatenate(
        [first_half * cosine - second_half * sine, second_half * cosine + first_half * sine],
        axis=-1,
    )


def rotate_back(grads, cosine, sine):
    return rotate(grads, cosine, -sine)


def dot_f32(left, right, dims):
    return lax.dot_general(left, right, (dims, ((), ())), preferred_element_type=jnp.float32)


def contract_rows(left, right):
    return dot_f32(left, right, ((0,), (0,)))


def contract_cols(left, right):
    return dot_f32(left, right, ((1,), (1,)))


def norm_back(upstream, unit, inverse, gain):
    scaled = upstream * gain
    gain_term = jnp.sum(upstream * unit, axis=0)
    input_term = inverse * (scaled - unit * jnp.mean(scaled * unit, axis=-1, keepdims=True))
    return (gain_term, input_term)


def local(
    tokens,
    segments,
    gain_one,
    query_w,
    query_b,
    key_w,
    key_b,
    value_w,
    value_b,
    out_w,
    gain_two,
    gate_w,
    up_w,
    down_w,
    cotangent,
):
    bf16, f32 = (jnp.bfloat16, jnp.float32)
    model_width = tokens.shape[1]
    rows = tokens.shape[0]
    tensor_size = lax.axis_size("tensor")
    rank = lax.axis_index("tensor")
    seq_length = rows * tensor_size
    kv_width = key_w.shape[1]
    query_width = query_w.shape[1] * tensor_size
    heads = query_width // HEAD_DIM
    group = heads // KV_HEADS
    scale = HEAD_DIM ** (-0.5)
    pair = lax.all_gather(jnp.stack([query_w, out_w]), "tensor", axis=2, tiled=True)
    joined = jnp.concatenate([pair[0], key_w, value_w, pair[1]], axis=1)
    joined = lax.all_gather(joined, "dp", axis=0, tiled=True)
    qkv_width = query_width + 2 * kv_width
    qkv_w = joined[:, :qkv_width]
    out_full = joined[:, qkv_width:]
    gains = lax.all_gather(jnp.stack([gain_one, gain_two]), "dp", axis=1, tiled=True).astype(f32)
    full_query_b = lax.all_gather(query_b, "tensor", axis=0, tiled=True)
    qkv_b = jnp.concatenate([full_query_b, key_b, value_b]).astype(f32)
    full_gate = lax.all_gather(gate_w, "dp", axis=0, tiled=True)
    full_up = lax.all_gather(up_w, "dp", axis=0, tiled=True)
    full_down = lax.all_gather(down_w, "dp", axis=0, tiled=True)
    cot_rows = lax.all_gather(cotangent, "tensor", axis=0, tiled=True)
    inputs = tokens.astype(f32)
    inverse_one = lax.rsqrt(jnp.mean(inputs * inputs, axis=-1, keepdims=True) + EPSILON)
    unit_one = inputs * inverse_one
    normed_one = (unit_one * gains[0]).astype(bf16)
    lin = jnp.dot(normed_one, qkv_w, preferred_element_type=f32) + qkv_b
    cosine, sine = angle_tables(rank * rows, rows, HEAD_DIM)
    cos_h, sin_h = (cosine[:, None, :], sine[:, None, :])
    query_rot = rotate(lin[:, :query_width].reshape(rows, heads, HEAD_DIM), cos_h, sin_h).astype(
        bf16
    )
    key_rot = rotate(
        lin[:, query_width : query_width + kv_width].reshape(rows, KV_HEADS, HEAD_DIM), cos_h, sin_h
    ).astype(bf16)
    value_own = lin[:, query_width + kv_width :].astype(bf16)
    kv_own = jnp.concatenate([key_rot.reshape(rows, kv_width), value_own], axis=1)
    kv_all = lax.all_gather(kv_own, "tensor", axis=0, tiled=True)
    window = min(seq_length, rows + -(-DOC_MAX // rows) * rows)
    first = jnp.maximum((rank + 1) * rows - window, 0)
    kv_win = lax.dynamic_slice_in_dim(kv_all, first, window, 0)
    key_win = kv_win[:, :kv_width].reshape(window, KV_HEADS, HEAD_DIM)
    value_win = kv_win[:, kv_width:].reshape(window, KV_HEADS, HEAD_DIM)
    segment = segments[0]
    own_segment = lax.dynamic_slice_in_dim(segment, rank * rows, rows, 0)
    win_segment = lax.dynamic_slice_in_dim(segment, first, window, 0)
    own_pos = rank * rows + jnp.arange(rows)
    win_pos = first + jnp.arange(window)
    allowed = (own_segment[:, None] == win_segment[None, :]) & (
        win_pos[None, :] <= own_pos[:, None]
    )
    grouped = query_rot.reshape(rows, KV_HEADS, group, HEAD_DIM)
    scores = jnp.einsum("tagd,sad->agts", grouped, key_win, preferred_element_type=f32) * scale
    masked = jnp.where(allowed, scores, NEGATIVE)
    largest = jnp.max(masked, axis=-1, keepdims=True)
    log_total = largest + jnp.log(jnp.sum(jnp.exp(masked - largest), axis=-1, keepdims=True))
    probs = jnp.exp(masked - log_total)
    probs_low = probs.astype(bf16)
    context = jnp.einsum("agts,sad->tagd", probs_low, value_win, preferred_element_type=f32)
    context = context.reshape(rows, query_width).astype(bf16)
    middle = inputs + contract_cols(context, out_full)
    inverse_two = lax.rsqrt(jnp.mean(middle * middle, axis=-1, keepdims=True) + EPSILON)
    unit_two = middle * inverse_two
    normed_two = (unit_two * gains[1]).astype(bf16)
    rows_two = lax.all_gather(normed_two, "tensor", axis=0, tiled=True)
    gate = jnp.dot(rows_two, full_gate, preferred_element_type=f32)
    upper = jnp.dot(rows_two, full_up, preferred_element_type=f32)
    sigmoid = jax.nn.sigmoid(gate)
    hidden_low = (gate * sigmoid * upper).astype(bf16)
    ffn_sum = lax.psum_scatter(
        contract_cols(hidden_low, full_down).astype(bf16), "tensor", scatter_dimension=0, tiled=True
    ).astype(f32)
    mixed = (middle + ffn_sum).astype(bf16)
    d_hidden = jnp.dot(cot_rows, full_down, preferred_element_type=f32)
    d_upper = (d_hidden * gate * sigmoid).astype(bf16)
    d_gate = (d_hidden * upper * sigmoid * (1.0 + gate * (1.0 - sigmoid))).astype(bf16)
    d_normed_two = lax.psum_scatter(
        (contract_cols(d_gate, full_gate) + contract_cols(d_upper, full_up)).astype(bf16),
        "tensor",
        scatter_dimension=0,
        tiled=True,
    ).astype(f32)
    grad_down = contract_rows(cot_rows, hidden_low).astype(bf16)
    grad_gate = contract_rows(rows_two, d_gate).astype(bf16)
    grad_up = contract_rows(rows_two, d_upper).astype(bf16)
    gain_two_term, d_from_two = norm_back(d_normed_two, unit_two, inverse_two, gains[1])
    d_middle = cotangent.astype(f32) + d_from_two
    d_attended = d_middle.astype(bf16)
    d_context = jnp.dot(d_attended, out_full, preferred_element_type=f32).astype(bf16)
    grad_out = contract_rows(d_attended, context).astype(bf16)
    d_context = d_context.reshape(rows, KV_HEADS, group, HEAD_DIM)
    d_probs = jnp.einsum("tagd,sad->agts", d_context, value_win, preferred_element_type=f32)
    row_delta = jnp.sum(probs * d_probs, axis=-1, keepdims=True)
    d_scores = (probs * (d_probs - row_delta)).astype(bf16)
    d_query_rot = (
        jnp.einsum("agts,sad->tagd", d_scores, key_win, preferred_element_type=f32) * scale
    )
    d_key_win = jnp.einsum("agts,tagd->sad", d_scores, grouped, preferred_element_type=f32) * scale
    d_value_win = jnp.einsum("agts,tagd->sad", probs_low, d_context, preferred_element_type=f32)
    d_query_lin = (
        rotate_back(d_query_rot.reshape(rows, heads, HEAD_DIM), cos_h, sin_h)
        .reshape(rows, query_width)
        .astype(bf16)
    )
    d_kv_win = jnp.concatenate(
        [d_key_win.reshape(window, kv_width), d_value_win.reshape(window, kv_width)], axis=1
    ).astype(bf16)
    d_kv_all = lax.dynamic_update_slice(
        jnp.zeros((seq_length, 2 * kv_width), bf16), d_kv_win, (first, 0)
    )
    d_kv = lax.psum_scatter(d_kv_all, "tensor", scatter_dimension=0, tiled=True).astype(f32)
    d_key_lin = rotate_back(d_kv[:, :kv_width].reshape(rows, KV_HEADS, HEAD_DIM), cos_h, sin_h)
    d_lin = jnp.concatenate(
        [
            d_query_lin,
            d_key_lin.reshape(rows, kv_width).astype(bf16),
            d_kv[:, kv_width:].astype(bf16),
        ],
        axis=1,
    )
    d_normed_one = contract_cols(d_lin, qkv_w)
    grad_qkv = contract_rows(normed_one, d_lin).astype(bf16)
    bias_term = jnp.sum(d_lin.astype(f32), axis=0)
    gain_one_term, d_from_one = norm_back(d_normed_one, unit_one, inverse_one, gains[0])
    input_grad = (d_middle + d_from_one).astype(bf16)

    def over_dp(grad):
        return lax.psum_scatter(grad, "dp", scatter_dimension=0, tiled=True)

    sum_gate, sum_up, sum_down = (over_dp(g).astype(f32) for g in (grad_gate, grad_up, grad_down))
    part = over_dp(jnp.concatenate([grad_qkv, grad_out], axis=1))
    pair = jnp.stack([part[:, :query_width], part[:, qkv_width:]])
    pair = lax.psum_scatter(pair, "tensor", scatter_dimension=2, tiled=True).astype(f32)
    kv_part = lax.psum_scatter(
        part[:, query_width:qkv_width], "tensor", scatter_dimension=0, tiled=True
    ).astype(f32)
    small = lax.psum(jnp.concatenate([bias_term, gain_one_term, gain_two_term]), ("dp", "tensor"))
    place = lax.axis_index("dp") * tensor_size + rank
    devices = lax.axis_size("dp") * tensor_size

    def own(start, size):
        share = size // devices
        return lax.dynamic_slice_in_dim(small, start + place * share, share, 0)

    return (
        mixed,
        input_grad,
        own(qkv_width, model_width),
        pair[0],
        own(0, query_width),
        kv_part[:, :kv_width],
        small[query_width : query_width + kv_width],
        kv_part[:, kv_width:],
        small[query_width + kv_width : qkv_width],
        pair[1],
        own(qkv_width + model_width, model_width),
        sum_gate,
        sum_up,
        sum_down,
    )


def solution(mesh):
    both = ("dp", "tensor")
    return jax.shard_map(
        local,
        mesh=mesh,
        in_specs=(
            P(both, None),
            P("dp", None),
            P("dp"),
            P("dp", "tensor"),
            P("tensor"),
            P("dp", None),
            P(),
            P("dp", None),
            P(),
            P("dp", "tensor"),
            P("dp"),
            P("dp", "tensor"),
            P("dp", "tensor"),
            P("dp", "tensor"),
            P(both, None),
        ),
        out_specs=(
            P(both, None),
            P(both, None),
            P(both),
            P("dp", "tensor"),
            P(both),
            P(both, None),
            P(),
            P(both, None),
            P(),
            P("dp", "tensor"),
            P(both),
            P("dp", "tensor"),
            P("dp", "tensor"),
            P("dp", "tensor"),
        ),
        check_vma=False,
    )
```

profile of v0, /device:TPU:0, one launch (start us, length us, event | category | flops | bytes accessed | tf_op | source)
XLA Modules:
  0.0 1033.9 jit_solution(3349695426935198296)
XLA Ops:
  7.3 1.8 pad_maximum_fusion.7
  9.2 34.0 %all-gather.11.cloned.1.call-done = bf16[2,192,1536]{2,1,0:T(8,128)(2,1)} async-done(((bf16[2,192,384]{2,1,0:T(8,128)(2,1)}), bf16[2,192,1536]{2,1,0:T(8,128)(2,1)}) %all-gather.11.cloned.1.call-update) | async-done | bytes 1179664 | tf_op jit(solution)/shard_map/all_gather | solution.py:83
  44.5 2.1 pad_maximum_fusion.1
  46.7 8.9 all-gather
  55.7 11.9 %all-gather.1 = bf16[4,1,384]{2,1,0:T(2,128)(2,1)S(1)} all-gather(bf16[1,1,384]{2,1,0:T(2,128)(2,1)S(1)} %reshape.237), channel_id=1, replica_groups=mesh['dp'=8,'tensor'=4] {'tensor'}, dimensions={0}, use_global_device_ids=true | all-gather | bytes 3840 | tf_op jit(solution)/shard_map/all_gather | solution.py:90
  69.2 42.2 %all-gather.13.cloned.1.call-done = bf16[1536,3584]{1,0:T(8,128)(2,1)} async-done(((bf16[192,3584]{1,0:T(8,128)(2,1)}), bf16[1536,3584]{1,0:T(8,128)(2,1)}) %all-gather.13.cloned.1.call-update) | async-done | bytes 11010064 | tf_op jit(solution)/shard_map/all_gather | solution.py:85
  111.4 4.7 fusion.17
  120.7 2.7 slice.133
  123.4 1.9 copy.118
  126.3 21.2 %all-gather.15.cloned.1.call-done = bf16[1024,512]{1,0:T(8,128)(2,1)} async-done(((bf16[256,512]{1,0:T(8,128)(2,1)}), bf16[1024,512]{1,0:T(8,128)(2,1)}) %all-gather.15.cloned.1.call-update) | async-done | bytes 1048592 | tf_op jit(solution)/shard_map/all_gather | solution.py:111
  147.5 2.1 constant_dynamic-slice_fusion.1
  151.3 2.4 fusion.9
  153.7 1.9 exponential_reduce_fusion
  155.6 2.1 copy-done.2
  157.7 2.4 convolution_convert_fusion.6
  160.1 4.2 multiply_reduce_fusion
  168.2 29.2 %all-gather.19.cloned.1.call-done = bf16[1536,2240]{1,0:T(8,128)(2,1)} async-done(((bf16[192,2240]{1,0:T(8,128)(2,1)}), bf16[1536,2240]{1,0:T(8,128)(2,1)}) %all-gather.19.cloned.1.call-update) | async-done | bytes 6881296 | tf_op jit(solution)/shard_map/all_gather | solution.py:92
  197.4 65.5 %all-gather.17.cloned.1.call-done = bf16[1024,1536]{1,0:T(8,128)(2,1)} async-done(((bf16[256,1536]{1,0:T(8,128)(2,1)}), bf16[1024,1536]{1,0:T(8,128)(2,1)}) %all-gather.17.cloned.1.call-update) | async-done | bytes 3145744 | tf_op jit(solution)/shard_map/all_gather | solution.py:138
  262.8 13.2 %fusion.67 = f32[1024,2240]{0,1:T(8,128)} fusion(bf16[1024,1536]{1,0:T(8,128)(2,1)} %all-gather.17.cloned.1.call-done, bf16[1536,2240]{1,0:T(8,128)(2,1)} %all-gather.19.cloned.1.call-done), kind=kOutput, calls=%fused_computation.132 | convolution fusion | flops 7046430720 | bytes 19202048 | tf_op jit(solution)/shard_map/dot_general | solution.py:139
  276.0 35.9 %all-gather.21.cloned.1.call-done = bf16[1536,2240]{1,0:T(8,128)(2,1)} async-done(((bf16[192,2240]{1,0:T(8,128)(2,1)}), bf16[1536,2240]{1,0:T(8,128)(2,1)}) %all-gather.21.cloned.1.call-update) | async-done | bytes 6881296 | tf_op jit(solution)/shard_map/all_gather | solution.py:93
  312.0 13.3 %fusion.68 = f32[1024,2240]{0,1:T(8,128)} fusion(bf16[1024,1536]{1,0:T(8,128)(2,1)} %all-gather.17.cloned.1.call-done, bf16[1536,2240]{1,0:T(8,128)(2,1)} %all-gather.21.cloned.1.call-done), kind=kOutput, calls=%fused_computation.133 | convolution fusion | flops 7046430720 | bytes 19202048 | tf_op jit(solution)/shard_map/dot_general | solution.py:140
  325.3 51.8 %all-gather.25.cloned.1.call-done = bf16[1024,1536]{1,0:T(8,128)(2,1)} async-done(((bf16[256,1536]{1,0:T(8,128)(2,1)}), bf16[1024,1536]{1,0:T(8,128)(2,1)}) %all-gather.25.cloned.1.call-update) | async-done | bytes 3145744 | tf_op jit(solution)/shard_map/all_gather | solution.py:95
  377.0 49.3 %all-gather.23.cloned.1.call-done = bf16[1536,2240]{1,0:T(8,128)(2,1)} async-done(((bf16[192,2240]{1,0:T(8,128)(2,1)}), bf16[1536,2240]{1,0:T(8,128)(2,1)}) %all-gather.23.cloned.1.call-update) | async-done | bytes 6881296 | tf_op jit(solution)/shard_map/all_gather | solution.py:94
  426.3 20.5 %multiply_convert_fusion = (bf16[1024,2240]{0,1:T(8,128)(2,1)}, bf16[1024,2240]{0,1:T(8,128)(2,1)}, bf16[1024,2240]{0,1:T(8,128)(2,1)}) fusion(f32[1024,2240]{0,1:T(8,128)} %fusion.67, f32[1024,2240]{0,1:T(8,128)} %fusion.68, bf16[1024,1536]{1,0:T(8,128)(2,1)} %all-gather.25.cloned.1.call-done, bf16[1536,2240]{1,0:T(8,128)(2,1)} %all-gather.23.cloned.1.call-done), kind=kOutput, calls=%fused_computation.13 | convolution fusion | flops 7083130880 | bytes 42139648 | tf_op jit(solution)/shard_map/dot_general | solution.py:147
  446.8 11.4 %fusion.69 = f32[1024,1536]{1,0:T(8,128)S(1)} fusion(bf16[1024,2240]{0,1:T(8,128)(2,1)} %get-tuple-element.91, bf16[1536,2240]{1,0:T(8,128)(2,1)} %all-gather.19.cloned.1.call-done), kind=kOutput, calls=%fused_computation.134 | convolution fusion | flops 7046430720 | bytes 17760256 | tf_op jit(solution)/shard_map/dot_general | solution.py:37
  458.2 9.4 add_convert_fusion
  467.7 12.5 %convolution_convert_fusion.5 = bf16[1024,1536]{1,0:T(8,128)(2,1)} fusion(bf16[1024,2240]{0,1:T(8,128)(2,1)} %get-tuple-element.92, bf16[1536,2240]{1,0:T(8,128)(2,1)} %all-gather.23.cloned.1.call-done), kind=kOutput, calls=%fused_computation.30 | convolution fusion | flops 7048003584 | bytes 14614528 | tf_op jit(solution)/shard_map/dot_general | solution.py:37
  480.2 48.0 %reduce-scatter.16.cloned.1.call-done = bf16[256,1536]{1,0:T(8,128)(2,1)} async-done(((bf16[1024,1536]{1,0:T(8,128)(2,1)}), bf16[256,1536]{1,0:T(8,128)(2,1)}) %reduce-scatter.16.cloned.1.call-update) | async-done | bytes 786448 | tf_op jit(solution)/shard_map/reduce_scatter | solution.py:150
  528.2 2.3 fusion.32
  530.5 60.1 %reduce-scatter.14.cloned.1.call-done = bf16[256,1536]{1,0:T(8,128)(2,1)} async-done(((bf16[1024,1536]{1,0:T(8,128)(2,1)}), bf16[256,1536]{1,0:T(8,128)(2,1)}) %reduce-scatter.14.cloned.1.call-update) | async-done | bytes 786448 | tf_op jit(solution)/shard_map/reduce_scatter | solution.py:143
  590.7 3.6 fusion.31
  594.3 4.7 fusion.20
  599.0 2.3 copy.124
  601.3 9.2 fusion.1
  610.5 6.2 fusion.43
  616.7 11.1 %fusion.3 = bf16[2,6,256,768]{2,3,1,0:T(8,128)(2,1)} fusion(f32[2,768,256,6]{2,1,3,0:T(8,128)} %get-tuple-element.130, f32[2,768,256,6]{2,1,3,0:T(8,128)} %copy-done.2, f32[2,6,256]{2,1,0:T(8,128)S(1)} %get-tuple-element.129, f32[2,6,256]{2,1,0:T(8,128)S(1)} %copy-done.17, pred[256,768]{0,1:T(8,128)(4,1)S(1)} %compare_and_fusion), kind=kLoop, calls=%fused_computation.9 | loop fusion | flops 14155776 | bytes 23814144 | tf_op jit(solution)/shard_map/convert_element_type | solution.py:167
  627.9 4.7 fusion.42
  634.6 7.8 dynamic_update_slice.3
  643.5 3.2 convolution_multiply_fusion
  647.9 3.6 convolution_convert_fusion.4
  651.5 18.4 %reduce-scatter.18.cloned.1.call-done = bf16[256,512]{0,1:T(8,128)(2,1)} async-done(((bf16[1024,512]{0,1:T(8,128)(2,1)}), bf16[256,512]{0,1:T(8,128)(2,1)}) %reduce-scatter.18.cloned.1.call-update) | async-done | bytes 262160 | tf_op jit(solution)/shard_map/reduce_scatter | solution.py:184
  672.9 3.2 convolution_convert_fusion.3
  676.2 5.2 pad_maximum_fusion
  681.4 12.3 %fusion = bf16[1536,2240]{0,1:T(8,128)(2,1)} fusion(bf16[1024,2240]{0,1:T(8,128)(2,1)} %get-tuple-element.92, bf16[1024,1536]{1,0:T(8,128)(2,1)} %all-gather.25.cloned.1.call-done), kind=kOutput, calls=%fused_computation.4 | convolution fusion | flops 7049871360 | bytes 14614528 | tf_op jit(solution)/shard_map/dot_general | solution.py:37
  693.7 10.7 %copy.161 = bf16[1536,2240]{1,0:T(8,128)(2,1)} copy(bf16[1536,2240]{0,1:T(8,128)(2,1)} %fusion) | data formatting | bytes 13762560
  704.7 12.3 %convolution_convert_fusion.2 = bf16[1536,2240]{1,0:T(8,128)(2,1)} fusion(bf16[1024,1536]{1,0:T(8,128)(2,1)} %all-gather.17.cloned.1.call-done, bf16[1024,2240]{0,1:T(8,128)(2,1)} %get-tuple-element.91), kind=kOutput, calls=%fused_computation.2 | convolution fusion | flops 7049871360 | bytes 14614528 | tf_op jit(solution)/shard_map/dot_general | solution.py:37
  717.1 12.7 %convolution_convert_fusion.1 = bf16[1536,2240]{1,0:T(8,128)(2,1)} fusion(bf16[1024,1536]{1,0:T(8,128)(2,1)} %all-gather.17.cloned.1.call-done, bf16[1024,2240]{0,1:T(8,128)(2,1)} %get-tuple-element.90), kind=kOutput, calls=%fused_computation.1 | convolution fusion | flops 7049871360 | bytes 14614528 | tf_op jit(solution)/shard_map/dot_general | solution.py:37
  729.8 34.6 %reduce-scatter.20.cloned.1.call-done = bf16[192,3584]{1,0:T(8,128)(2,1)} async-done(((bf16[1536,3584]{1,0:T(8,128)(2,1)}), bf16[192,3584]{1,0:T(8,128)(2,1)}) %reduce-scatter.20.cloned.1.call-update) | async-done | bytes 1376272 | tf_op jit(solution)/shard_map/reduce_scatter | solution.py:201
  764.4 1.6 slice.147
  768.8 4.8 copy.159
  773.6 4.6 reshape.246
  778.3 1.6 convert_reduce_fusion
  779.9 7.1 fusion.39
  787.0 40.5 %psum.7 = f32[5120]{0:T(1024)S(1)} all-reduce(f32[5120]{0:T(1024)S(1)} %pad_maximum_fusion.13), channel_id=1, replica_groups=mesh['dp'=8,'tensor'=4] {'dp','tensor'}, use_global_device_ids=true, to_apply=%region_13.14 | all-reduce | flops 5120 | bytes 40960 | tf_op jit(solution)/shard_map/psum | solution.py:210
  828.7 2.8 fusion.38
  831.4 2.9 reduce-scatter.30.cloned.1.call-done
  834.3 1.7 copy.162
  836.1 1.7 copy.137
  837.8 65.5 %reduce-scatter.24.cloned.1.call-done = bf16[192,2240]{1,0:T(8,128)(2,1)} async-done(((bf16[1536,2240]{1,0:T(8,128)(2,1)}), bf16[192,2240]{1,0:T(8,128)(2,1)}) %reduce-scatter.24.cloned.1.call-update) | async-done | bytes 860176 | tf_op jit(solution)/shard_map/reduce_scatter | solution.py:201
  903.2 2.5 convert_element_type.164
  905.7 66.4 %reduce-scatter.26.cloned.1.call-done = bf16[192,2240]{1,0:T(8,128)(2,1)} async-done(((bf16[1536,2240]{1,0:T(8,128)(2,1)}), bf16[192,2240]{1,0:T(8,128)(2,1)}) %reduce-scatter.26.cloned.1.call-update) | async-done | bytes 860176 | tf_op jit(solution)/shard_map/reduce_scatter | solution.py:201
  972.1 2.5 convert_element_type.166
  974.6 19.8 %reduce-scatter.22.cloned.1.call-done = bf16[48,512]{1,0:T(8,128)(2,1)} async-done(((bf16[192,512]{1,0:T(8,128)(2,1)}), bf16[48,512]{1,0:T(8,128)(2,1)}) %reduce-scatter.22.cloned.1.call-update) | async-done | bytes 49168 | tf_op jit(solution)/shard_map/reduce_scatter | solution.py:207
  995.8 28.4 %reduce-scatter.28.cloned.1.call-done = bf16[384,384]{1,0:T(8,128)(2,1)} async-done(((bf16[1536,384]{1,0:T(8,128)(2,1)}), bf16[384,384]{1,0:T(8,128)(2,1)}) %reduce-scatter.28.cloned.1.call-update) | async-done | bytes 294928
  (160 shorter events, 30.0 us)
Async XLA Ops:
  7.2 113.1 %copy-start = (s32[1,1024]{1,0:T(1,128)S(1)}, s32[1,1024]{1,0:T(1,128)}, u32[]{:S(2)}) copy-start(s32[1,1024]{1,0:T(1,128)} %param.16) | copy-start | bytes 12292
  7.2 39.5 %copy-start.27 = (bf16[192]{0:T(256)(128)(2,1)S(1)}, bf16[192]{0:T(256)(128)(2,1)}, u32[]{:S(2)}) copy-start(bf16[192]{0:T(256)(128)(2,1)} %param.17) | copy-start | bytes 1156
  7.2 39.5 %copy-start.28 = (bf16[192]{0:T(256)(128)(2,1)S(1)}, bf16[192]{0:T(256)(128)(2,1)}, u32[]{:S(2)}) copy-start(bf16[192]{0:T(256)(128)(2,1)} %param.25) | copy-start | bytes 1156
  7.2 48.5 %copy-start.23 = (bf16[384]{0:T(512)(128)(2,1)S(1)}, bf16[384]{0:T(512)(128)(2,1)}, u32[]{:S(2)}) copy-start(bf16[384]{0:T(512)(128)(2,1)} %param.19) | copy-start | bytes 2308
  7.2 61.6 %copy-start.25 = (bf16[256]{0:T(256)(128)(2,1)S(1)}, bf16[256]{0:T(256)(128)(2,1)}, u32[]{:S(2)}) copy-start(bf16[256]{0:T(256)(128)(2,1)} %param.21) | copy-start | bytes 1540
  7.2 61.6 %copy-start.24 = (bf16[256]{0:T(256)(128)(2,1)S(1)}, bf16[256]{0:T(256)(128)(2,1)}, u32[]{:S(2)}) copy-start(bf16[256]{0:T(256)(128)(2,1)} %param.23) | copy-start | bytes 1540
  7.2 61.7 %copy-start.4 = (bf16[256,1536]{1,0:T(8,128)(2,1)S(1)}, bf16[256,1536]{1,0:T(8,128)(2,1)}, u32[]{:S(2)}) copy-start(bf16[256,1536]{1,0:T(8,128)(2,1)} %param.15) | copy-start | bytes 2359300
  7.3 35.9 %all-gather.11.cloned.1.call-start = ((), (), s32[]{:S(2)}) async-start(), calls=%async_computation.9 | async-start | bytes 1474560 | tf_op jit(solution)/shard_map/all_gather | solution.py:83
  9.1 102.3 %all-gather.13.cloned.1.call-start = ((), (), s32[]{:S(2)}) async-start(), calls=%async_computation.10 | async-start | bytes 12386304 | tf_op jit(solution)/shard_map/all_gather | solution.py:85
  46.6 100.9 %all-gather.15.cloned.1.call-start = ((), (), s32[]{:S(2)}) async-start(), calls=%async_computation.11 | async-start | bytes 1310720 | tf_op jit(solution)/shard_map/all_gather | solution.py:111
  68.7 49.0 %copy-start.11 = (f32[256,64]{1,0:T(8,128)}, f32[256,64]{1,0:T(8,128)S(1)}, u32[]{:S(2)}) copy-start(f32[256,64]{1,0:T(8,128)S(1)} %copy.116) | copy-start | bytes 196612
  68.9 47.2 %copy-start.18 = (f32[1536]{0:T(1024)}, f32[1536]{0:T(1024)S(1)}, u32[]{:S(2)}) copy-start(f32[1536]{0:T(1024)S(1)} %get-tuple-element.89) | copy-start | bytes 18436
  69.2 46.9 %copy-start.21 = (f32[256]{0:T(256)}, f32[256]{0:T(256)S(1)}, u32[]{:S(2)}) copy-start(f32[256]{0:T(256)S(1)} %add_rsqrt_fusion.1) | copy-start | bytes 3076
  116.1 1.4 copy-start.8
  119.4 78.0 %all-gather.19.cloned.1.call-start = ((), (), s32[]{:S(2)}) async-start(), calls=%async_computation.13 | async-start | bytes 7962624 | tf_op jit(solution)/shard_map/all_gather | solution.py:92
  120.0 142.9 %all-gather.17.cloned.1.call-start = ((), (), s32[]{:S(2)}) async-start(), calls=%async_computation.12 | async-start | bytes 3932160 | tf_op jit(solution)/shard_map/all_gather | solution.py:138
  125.9 27.7 %copy-start.5 = (bf16[256,12,64]{2,0,1:T(8,128)(2,1)}, bf16[256,12,64]{2,0,1:T(8,128)(2,1)S(1)}, u32[]{:S(2)}) copy-start(bf16[256,12,64]{2,0,1:T(8,128)(2,1)S(1)} %copy.119) | copy-start | bytes 1179652
  126.3 27.3 %copy-start.6 = (bf16[256,12,64]{2,0,1:T(8,128)(2,1)}, bf16[256,12,64]{2,0,1:T(8,128)(2,1)S(1)}, u32[]{:S(2)}) copy-start(bf16[256,12,64]{2,0,1:T(8,128)(2,1)S(1)} %copy.120) | copy-start | bytes 1179652
  151.3 4.3 copy-start.9
  153.6 4.0 copy-start.2
  155.6 4.5 copy-start.16
  160.1 4.2 copy-start.13
  164.3 363.9 %copy-start.3 = (f32[256,1536]{1,0:T(8,128)}, f32[256,1536]{1,0:T(8,128)S(1)}, u32[]{:S(2)}) copy-start(f32[256,1536]{1,0:T(8,128)S(1)} %get-tuple-element.128) | copy-start | bytes 4718596
  165.6 146.4 %all-gather.21.cloned.1.call-start = ((), (), s32[]{:S(2)}) async-start(), calls=%async_computation.14 | async-start | bytes 7962624 | tf_op jit(solution)/shard_map/all_gather | solution.py:93
  166.1 210.9 %all-gather.25.cloned.1.call-start = ((), (), s32[]{:S(2)}) async-start(), calls=%async_computation.17 | async-start | bytes 3932160 | tf_op jit(solution)/shard_map/all_gather | solution.py:95
  166.9 259.4 %all-gather.23.cloned.1.call-start = ((), (), s32[]{:S(2)}) async-start(), calls=%async_computation.15 | async-start | bytes 7962624 | tf_op jit(solution)/shard_map/all_gather | solution.py:94
  167.6 360.5 %reduce-scatter.16.cloned.1.call-start = ((), (), s32[]{:S(2)}) async-start(), calls=%async_computation.18 | async-start | bytes 3932160 | tf_op jit(solution)/shard_map/reduce_scatter | solution.py:150
  446.8 11.4 %copy-start.26 = (bf16[1536,2240]{1,0:T(8,128)(2,1)S(1)}, bf16[1536,2240]{1,0:T(8,128)(2,1)}, u32[]{:S(2)}) copy-start(bf16[1536,2240]{1,0:T(8,128)(2,1)} %all-gather.21.cloned.1.call-done) | copy-start | bytes 20643844
  446.8 11.4 %copy-start.29 = (bf16[1024,2240]{0,1:T(8,128)(2,1)S(1)}, bf16[1024,2240]{0,1:T(8,128)(2,1)}, u32[]{:S(2)}) copy-start(bf16[1024,2240]{0,1:T(8,128)(2,1)} %get-tuple-element.90) | copy-start | bytes 13762564
  467.6 123.0 %reduce-scatter.14.cloned.1.call-start = ((), (), s32[]{:S(2)}) async-start(), calls=%async_computation.16 | async-start | bytes 3932160 | tf_op jit(solution)/shard_map/reduce_scatter | solution.py:143
  480.1 189.7 %reduce-scatter.18.cloned.1.call-start = ((), (), s32[]{:S(2)}) async-start(), calls=%async_computation.19 | async-start | bytes 1310720 | tf_op jit(solution)/shard_map/reduce_scatter | solution.py:184
  594.3 7.0 copy-start.10
  594.3 7.0 copy-start.17
  601.2 9.2 copy-start.7
  627.9 14.8 %copy-start.15 = (f32[256,64]{0,1:T(8,128)S(1)}, f32[256,64]{0,1:T(8,128)}, u32[]{:S(2)}) copy-start(f32[256,64]{0,1:T(8,128)} %get-tuple-element.122) | copy-start | bytes 196612
  642.5 122.0 %reduce-scatter.20.cloned.1.call-start = ((), (), s32[]{:S(2)}) async-start(), calls=%async_computation.20 | async-start | bytes 12386304 | tf_op jit(solution)/shard_map/reduce_scatter | solution.py:201
  643.5 4.4 copy-start.14
  647.9 23.3 %copy-start.12 = (f32[256,64]{1,0:T(8,128)S(1)}, f32[256,64]{1,0:T(8,128)}, u32[]{:S(2)}) copy-start(f32[256,64]{1,0:T(8,128)} %copy-done.11) | copy-start | bytes 196612
  647.9 25.0 %copy-start.19 = (f32[1536]{0:T(1024)S(1)}, f32[1536]{0:T(1024)}, u32[]{:S(2)}) copy-start(f32[1536]{0:T(1024)} %copy-done.18) | copy-start | bytes 18436
  647.9 25.0 %copy-start.22 = (f32[256]{0:T(256)S(1)}, f32[256]{0:T(256)}, u32[]{:S(2)}) copy-start(f32[256]{0:T(256)} %copy-done.21) | copy-start | bytes 3076
  672.7 3.4 slice-start
  672.9 3.3 slice-start.1
  681.4 153.0 %reduce-scatter.30.cloned.1.call-start = ((), (), s32[]{:S(2)}) async-start(), calls=%async_computation.25 | async-start | bytes 7962624
  704.4 198.8 %reduce-scatter.24.cloned.1.call-start = ((), (), s32[]{:S(2)}) async-start(), calls=%async_computation.22 | async-start | bytes 7962624 | tf_op jit(solution)/shard_map/reduce_scatter | solution.py:201
  717.0 255.1 %reduce-scatter.26.cloned.1.call-start = ((), (), s32[]{:S(2)}) async-start(), calls=%async_computation.23 | async-start | bytes 7962624 | tf_op jit(solution)/shard_map/reduce_scatter | solution.py:201
  729.8 264.6 %reduce-scatter.22.cloned.1.call-start = ((), (), s32[]{:S(2)}) async-start(), calls=%async_computation.21 | async-start | bytes 245760 | tf_op jit(solution)/shard_map/reduce_scatter | solution.py:207
  766.1 258.1 %reduce-scatter.28.cloned.1.call-start = ((), (), s32[]{:S(2)}) async-start(), calls=%async_computation.24 | async-start | bytes 1474560
  779.9 7.1 copy-start.20
  836.1 191.0 %copy-start.1 = (s32[1,1024]{1,0:T(1,128)S(1)}, s32[1,1024]{1,0:T(1,128)}, u32[]{:S(2)}) copy-start(s32[1,1024]{1,0:T(1,128)} %param.16) | copy-start | bytes 12292
Sparse Core Ops, SparseCore 0:
  10.2 32.8 all-gather.10
  46.7 64.6 all-gather.12
  119.5 27.9 all-gather.14
  149.3 48.0 all-gather.18
  199.4 63.4 all-gather.16
  264.6 47.3 all-gather.20
  313.5 63.4 all-gather.24
  378.9 47.3 all-gather.22
  467.7 60.3 reduce-scatter.15
  530.3 60.3 reduce-scatter.13
  642.6 27.1 reduce-scatter.17
  681.5 82.8 reduce-scatter.19
  767.9 66.3 reduce-scatter.29
  837.7 65.4 reduce-scatter.23
  906.6 65.4 reduce-scatter.25
  974.8 19.5 reduce-scatter.21
  996.6 27.5 reduce-scatter.27
where the time goes:
time: 1040 us; the launch traced here: 1030 us
  waiting for transfers between devices  676 us (65%)
  matrix products  173 us (17%)
  blocking collectives  61.3 us (6%)
  local copies, waits for them, and re-layouts  59.8 us (6%)
  other arithmetic  46.9 us (5%)
  between operations  15 us (1%)
    reduce_scatter x3, waiting for transfers between devices, over_dp(): return lax.psum_scatter(grad, 'dp', scatter_dimension=0, tiled=True)  166 us
    dot_general x10, matrix products, dot_f32(): lax.dot_general(left, right, (dims, ((), ())), preferred_element_type=jnp...  88.6 us
    all_gather x1, waiting for transfers between devices, local(): rows_two = lax.all_gather(normed_two, 'tensor', axis=0, tiled=True)  65.5 us
    reduce_scatter x1, waiting for transfers between devices, local(): lax.psum_scatter(contract_cols(hidden_low, full_down).astype(bf16), 'tens...  60.1 us
    all_gather x1, waiting for transfers between devices, local(): cot_rows = lax.all_gather(cotangent, 'tensor', axis=0, tiled=True)  51.8 us
    all_gather x1, waiting for transfers between devices, local(): full_down = lax.all_gather(down_w, 'dp', axis=0, tiled=True)  49.3 us
    reduce_scatter x1, waiting for transfers between devices, local(): lax.psum_scatter((contract_cols(d_gate, full_gate) + contract_cols(d_uppe...  48 us
    all_gather x1, waiting for transfers between devices, local(): joined = lax.all_gather(joined, 'dp', axis=0, tiled=True)  42.2 us
  transfers between devices with their start and end apart: 17, of which 17 were waited for; matrix products, arithmetic and copies ran while one was open for 15% of the time, Pallas kernels for 0%

commit v1 on v0

--- a/solution.py
+++ b/solution.py
@@ -9,6 +9,19 @@
 EPSILON = 1e-06
 ROPE_BASE = 1000000.0
 NEGATIVE = -1e30
+
+
+def ring_gather(shard, axis, dim):
+    ways = lax.axis_size(axis)
+    up = [(d, (d + 1) % ways) for d in range(ways)]
+    down = [(d, (d - 1) % ways) for d in range(ways)]
+    earlier, later = ([shard], [shard])
+    for _ in range(ways // 2):
+        earlier.append(lax.ppermute(earlier[-1], axis, up))
+    for _ in range((ways - 1) // 2):
+        later.append(lax.ppermute(later[-1], axis, down))
+    line = jnp.concatenate([*earlier[::-1], *later[1:]], axis=dim)
+    return jnp.roll(line, (lax.axis_index(axis) - ways // 2) * shard.shape[dim], axis=dim)
 
 
 def angle_tables(first, length, head_width):
@@ -92,7 +105,7 @@
     full_gate = lax.all_gather(gate_w, "dp", axis=0, tiled=True)
     full_up = lax.all_gather(up_w, "dp", axis=0, tiled=True)
     full_down = lax.all_gather(down_w, "dp", axis=0, tiled=True)
-    cot_rows = lax.all_gather(cotangent, "tensor", axis=0, tiled=True)
+    cot_rows = ring_gather(cotangent, "tensor", 0)
     inputs = tokens.astype(f32)
     inverse_one = lax.rsqrt(jnp.mean(inputs * inputs, axis=-1, keepdims=True) + EPSILON)
     unit_one = inputs * inverse_one

time: 1040 us -> 988 us (0.950)
  waiting for transfers between devices: 676 us -> 614 us
    ppermute x0 -> x3, waiting for transfers between devices: none -> 72.9 us  [the longest x2 37.6 us: ring_gather(): earlier.append(lax.ppermute(earlier[-1], axis, up))]
    all_gather x1, waiting for transfers between devices: 65.5 us -> 12.8 us  [local(): rows_two = lax.all_gather(normed_two, 'tensor', axis=0, tiled=True)]
    all_gather x1 -> x0, waiting for transfers between devices: 51.8 us -> none  [local(): cot_rows = lax.all_gather(cotangent, 'tensor', axis=0, tiled=True)]
    all_gather x1, waiting for transfers between devices: 29.2 us -> 0.01 us  [local(): full_gate = lax.all_gather(gate_w, 'dp', axis=0, tiled=True)]
    reduce_scatter x3 -> x4, waiting for transfers between devices: 166 us -> 180 us  [over_dp(): return lax.psum_scatter(grad, 'dp', scatter_dimension=0, tiled=True)]
    all_gather x1, waiting for transfers between devices: 49.3 us -> 37.4 us  [local(): full_down = lax.all_gather(down_w, 'dp', axis=0, tiled=True)]
    unnamed x19 -> x17, waiting for transfers between devices: 33.9 us -> 30.3 us
    unnamed x76 -> x82, local copies, waits for them, and re-layouts: 29.4 us -> 28.7 us
  transfers between devices with their start and end apart: 17 -> 19, of which waited for: 17 -> 18; matrix products, arithmetic and copies ran while one was open for 15% -> 17% of each run, Pallas kernels for 0% -> 0%
where the time goes in v1:
time: 988 us; the launch traced here: 983 us
  waiting for transfers between devices  614 us (62%)
  matrix products  175 us (18%)
  blocking collectives  61.4 us (6%)
  local copies, waits for them, and re-layouts  61.2 us (6%)
  other arithmetic  49.4 us (5%)
  between operations  15 us (2%)
    reduce_scatter x4, waiting for transfers between devices, over_dp(): return lax.psum_scatter(grad, 'dp', scatter_dimension=0, tiled=True)  180 us
    dot_general x10, matrix products, dot_f32(): lax.dot_general(left, right, (dims, ((), ())), preferred_element_type=jnp...  89.8 us
    reduce_scatter x1, waiting for transfers between devices, local(): lax.psum_scatter(contract_cols(hidden_low, full_down).astype(bf16), 'tens...  60.3 us
    reduce_scatter x1, waiting for transfers between devices, local(): lax.psum_scatter((contract_cols(d_gate, full_gate) + contract_cols(d_uppe...  47.9 us
    all_gather x1, waiting for transfers between devices, local(): joined = lax.all_gather(joined, 'dp', axis=0, tiled=True)  42.2 us
    psum x1, blocking collectives, local(): lax.psum(jnp.concatenate([bias_term, gain_one_term, gain_two_term]), ('dp...  40.6 us
    ppermute x2, waiting for transfers between devices, ring_gather(): earlier.append(lax.ppermute(earlier[-1], axis, up))  37.6 us
    all_gather x1, waiting for transfers between devices, local(): full_down = lax.all_gather(down_w, 'dp', axis=0, tiled=True)  37.4 us
  transfers between devices with their start and end apart: 19, of which 18 were waited for; matrix products, arithmetic and copies ran while one was open for 17% of the time, Pallas kernels for 0%

profile of v1, /device:TPU:0, one launch (start us, length us, event | category | flops | bytes accessed | tf_op | source)
XLA Modules:
  0.0 982.8 jit_solution(1486486138218312664)
XLA Ops:
  9.2 34.0 %all-gather.10.cloned.1.call-done = bf16[2,192,1536]{2,1,0:T(8,128)(2,1)} async-done(((bf16[2,192,384]{2,1,0:T(8,128)(2,1)}), bf16[2,192,1536]{2,1,0:T(8,128)(2,1)}) %all-gather.10.cloned.1.call-update) | async-done | bytes 1179664 | tf_op jit(solution)/shard_map/all_gather | solution.py:96
  44.5 2.1 pad_maximum_fusion.1
  46.7 8.9 all-gather
  55.7 11.9 %all-gather.1 = bf16[4,1,384]{2,1,0:T(2,128)(2,1)S(1)} all-gather(bf16[1,1,384]{2,1,0:T(2,128)(2,1)S(1)} %reshape.237), channel_id=1, replica_groups=mesh['dp'=8,'tensor'=4] {'tensor'}, dimensions={0}, use_global_device_ids=true | all-gather | bytes 3840 | tf_op jit(solution)/shard_map/all_gather | solution.py:103
  69.2 42.2 %all-gather.12.cloned.1.call-done = bf16[1536,3584]{1,0:T(8,128)(2,1)} async-done(((bf16[192,3584]{1,0:T(8,128)(2,1)}), bf16[1536,3584]{1,0:T(8,128)(2,1)}) %all-gather.12.cloned.1.call-update) | async-done | bytes 11010064 | tf_op jit(solution)/shard_map/all_gather | solution.py:98
  111.4 4.7 fusion.19
  120.7 2.7 slice.133
  126.3 21.2 %all-gather.14.cloned.1.call-done = bf16[1024,512]{1,0:T(8,128)(2,1)} async-done(((bf16[256,512]{1,0:T(8,128)(2,1)}), bf16[1024,512]{1,0:T(8,128)(2,1)}) %all-gather.14.cloned.1.call-update) | async-done | bytes 1048592 | tf_op jit(solution)/shard_map/all_gather | solution.py:124
  147.5 2.1 constant_dynamic-slice_fusion.1
  151.3 2.4 fusion.8
  155.6 2.1 copy-done.2
  157.7 2.4 convolution_convert_fusion.6
  160.1 4.2 multiply_reduce_fusion
  168.3 19.4 %collective-permute-done = bf16[256,1536]{1,0:T(8,128)(2,1)} collective-permute-done((bf16[256,1536]{1,0:T(8,128)(2,1)}, bf16[256,1536]{1,0:T(8,128)(2,1)}, u32[]{:S(2)}, u32[]{:S(2)}) %collective-permute-start) | collective-permute-done | bytes 786464 | tf_op jit(solution)/shard_map/ppermute | solution.py:20
  187.6 4.3 collective-permute-start.2
  192.0 18.2 %collective-permute-done.1 = bf16[256,1536]{1,0:T(8,128)(2,1)} collective-permute-done((bf16[256,1536]{1,0:T(8,128)(2,1)}, bf16[256,1536]{1,0:T(8,128)(2,1)}, u32[]{:S(2)}, u32[]{:S(2)}) %collective-permute-start.1) | collective-permute-done | bytes 786464 | tf_op jit(solution)/shard_map/ppermute | solution.py:20
  214.3 2.1 constant_dynamic-update-slice_fusion.5
  216.4 35.3 %collective-permute-done.2 = bf16[256,1536]{1,0:T(8,128)(2,1)} collective-permute-done((bf16[256,1536]{1,0:T(8,128)(2,1)}, bf16[256,1536]{1,0:T(8,128)(2,1)}, u32[]{:S(2)}, u32[]{:S(2)}) %collective-permute-start.2) | collective-permute-done | bytes 786464 | tf_op jit(solution)/shard_map/ppermute | solution.py:22
  251.6 2.1 constant_dynamic-update-slice_fusion.4
  253.7 2.1 constant_dynamic-update-slice_fusion.3
  255.8 2.1 constant_dynamic-update-slice_fusion.2
  258.9 2.1 constant_dynamic-update-slice_fusion
  261.0 12.8 %all-gather.16.cloned.1.call-done = bf16[1024,1536]{1,0:T(8,128)(2,1)} async-done(((bf16[256,1536]{1,0:T(8,128)(2,1)}), bf16[1024,1536]{1,0:T(8,128)(2,1)}) %all-gather.16.cloned.1.call-update) | async-done | bytes 3145744 | tf_op jit(solution)/shard_map/all_gather | solution.py:151
  273.8 13.2 %fusion.71 = f32[1024,2240]{0,1:T(8,128)} fusion(bf16[1024,1536]{1,0:T(8,128)(2,1)} %all-gather.16.cloned.1.call-done, bf16[1536,2240]{1,0:T(8,128)(2,1)} %all-gather.18.cloned.1.call-done), kind=kOutput, calls=%fused_computation.144 | convolution fusion | flops 7046430720 | bytes 19202048 | tf_op jit(solution)/shard_map/dot_general | solution.py:152
  287.0 37.2 %all-gather.20.cloned.1.call-done = bf16[1536,2240]{1,0:T(8,128)(2,1)} async-done(((bf16[192,2240]{1,0:T(8,128)(2,1)}), bf16[1536,2240]{1,0:T(8,128)(2,1)}) %all-gather.20.cloned.1.call-update) | async-done | bytes 6881296 | tf_op jit(solution)/shard_map/all_gather | solution.py:106
  324.2 13.2 %fusion.72 = f32[1024,2240]{0,1:T(8,128)} fusion(bf16[1024,1536]{1,0:T(8,128)(2,1)} %all-gather.16.cloned.1.call-done, bf16[1536,2240]{1,0:T(8,128)(2,1)} %all-gather.20.cloned.1.call-done), kind=kOutput, calls=%fused_computation.145 | convolution fusion | flops 7046430720 | bytes 19202048 | tf_op jit(solution)/shard_map/dot_general | solution.py:153
  337.4 37.4 %all-gather.22.cloned.1.call-done = bf16[1536,2240]{1,0:T(8,128)(2,1)} async-done(((bf16[192,2240]{1,0:T(8,128)(2,1)}), bf16[1536,2240]{1,0:T(8,128)(2,1)}) %all-gather.22.cloned.1.call-update) | async-done | bytes 6881296 | tf_op jit(solution)/shard_map/all_gather | solution.py:107
  374.8 20.9 %multiply_convert_fusion = (bf16[1024,2240]{0,1:T(8,128)(2,1)}, bf16[1024,2240]{0,1:T(8,128)(2,1)}, bf16[1024,2240]{0,1:T(8,128)(2,1)}) fusion(f32[1024,2240]{0,1:T(8,128)} %fusion.71, f32[1024,2240]{0,1:T(8,128)} %fusion.72, bf16[1536,2240]{1,0:T(8,128)(2,1)} %all-gather.22.cloned.1.call-done, bf16[2048,1536]{1,0:T(8,128)(2,1)} %constant_dynamic-update-slice_fusion, ...), kind=kOutput, calls=%fused_computation.12 | convolution fusion | flops 7083130880 | bytes 42336260 | tf_op jit(solution)/shard_map/dot_general | solution.py:160
  395.8 11.4 %fusion.73 = f32[1024,1536]{1,0:T(8,128)S(1)} fusion(bf16[1024,2240]{0,1:T(8,128)(2,1)} %get-tuple-element.21, bf16[1536,2240]{1,0:T(8,128)(2,1)} %all-gather.18.cloned.1.call-done), kind=kOutput, calls=%fused_computation.146 | convolution fusion | flops 7046430720 | bytes 17760256 | tf_op jit(solution)/shard_map/dot_general | solution.py:50
  407.2 9.3 add_convert_fusion
  416.5 12.4 %convolution_convert_fusion.5 = bf16[1024,1536]{1,0:T(8,128)(2,1)} fusion(bf16[1024,2240]{0,1:T(8,128)(2,1)} %get-tuple-element.22, bf16[1536,2240]{1,0:T(8,128)(2,1)} %all-gather.22.cloned.1.call-done), kind=kOutput, calls=%fused_computation.29 | convolution fusion | flops 7048003584 | bytes 14614528 | tf_op jit(solution)/shard_map/dot_general | solution.py:50
  429.0 47.9 %reduce-scatter.14.cloned.1.call-done = bf16[256,1536]{1,0:T(8,128)(2,1)} async-done(((bf16[1024,1536]{1,0:T(8,128)(2,1)}), bf16[256,1536]{1,0:T(8,128)(2,1)}) %reduce-scatter.14.cloned.1.call-update) | async-done | bytes 786448 | tf_op jit(solution)/shard_map/reduce_scatter | solution.py:163
  476.9 2.3 fusion.34
  479.3 60.3 %reduce-scatter.12.cloned.1.call-done = bf16[256,1536]{1,0:T(8,128)(2,1)} async-done(((bf16[1024,1536]{1,0:T(8,128)(2,1)}), bf16[256,1536]{1,0:T(8,128)(2,1)}) %reduce-scatter.12.cloned.1.call-update) | async-done | bytes 786448 | tf_op jit(solution)/shard_map/reduce_scatter | solution.py:156
  539.6 3.5 fusion.33
  543.1 4.7 fusion.22
  547.8 2.3 copy.120
  550.1 9.2 fusion
  559.3 6.2 fusion.45
  565.6 11.2 %fusion.2 = bf16[2,6,256,768]{2,3,1,0:T(8,128)(2,1)} fusion(f32[2,768,256,6]{2,1,3,0:T(8,128)} %get-tuple-element.60, f32[2,768,256,6]{2,1,3,0:T(8,128)} %copy-done.2, f32[2,6,256]{2,1,0:T(8,128)S(1)} %get-tuple-element.59, f32[2,6,256]{2,1,0:T(8,128)S(1)} %copy-done.18, pred[256,768]{0,1:T(8,128)(4,1)S(1)} %compare_and_fusion), kind=kLoop, calls=%fused_computation.8 | loop fusion | flops 14155776 | bytes 23814144 | tf_op jit(solution)/shard_map/convert_element_type | solution.py:180
  576.7 4.7 fusion.44
  583.5 7.8 dynamic_update_slice.3
  592.3 3.2 convolution_multiply_fusion
  596.7 3.6 convolution_convert_fusion.4
  600.3 18.3 %reduce-scatter.16.cloned.1.call-done = bf16[256,512]{0,1:T(8,128)(2,1)} async-done(((bf16[1024,512]{0,1:T(8,128)(2,1)}), bf16[256,512]{0,1:T(8,128)(2,1)}) %reduce-scatter.16.cloned.1.call-update) | async-done | bytes 262160 | tf_op jit(solution)/shard_map/reduce_scatter | solution.py:197
  621.7 3.2 convolution_convert_fusion.3
  625.0 5.2 pad_maximum_fusion
  630.2 12.7 %convolution_convert_fusion = bf16[1536,2240]{1,0:T(8,128)(2,1)} fusion(bf16[1024,2240]{0,1:T(8,128)(2,1)} %get-tuple-element.22, bf16[2048,1536]{1,0:T(8,128)(2,1)} %constant_dynamic-update-slice_fusion, s32[]{:T(128)S(6)} %select_n.35), kind=kOutput, calls=%fused_computation | convolution fusion | flops 7049871360 | bytes 14614532 | tf_op jit(solution)/shard_map/dot_general | solution.py:50
  643.2 13.6 %convolution_convert_fusion.2 = bf16[1536,2240]{1,0:T(8,128)(2,1)} fusion(bf16[1024,1536]{1,0:T(8,128)(2,1)} %all-gather.16.cloned.1.call-done, bf16[1024,2240]{0,1:T(8,128)(2,1)} %get-tuple-element.21), kind=kOutput, calls=%fused_computation.2 | convolution fusion | flops 7049871360 | bytes 14614528 | tf_op jit(solution)/shard_map/dot_general | solution.py:50
  656.9 12.4 %convolution_convert_fusion.1 = bf16[1536,2240]{1,0:T(8,128)(2,1)} fusion(bf16[1024,1536]{1,0:T(8,128)(2,1)} %all-gather.16.cloned.1.call-done, bf16[1024,2240]{0,1:T(8,128)(2,1)} %get-tuple-element.20), kind=kOutput, calls=%fused_computation.1 | convolution fusion | flops 7049871360 | bytes 14614528 | tf_op jit(solution)/shard_map/dot_general | solution.py:50
  669.4 43.9 %reduce-scatter.18.cloned.1.call-done = bf16[192,3584]{1,0:T(8,128)(2,1)} async-done(((bf16[1536,3584]{1,0:T(8,128)(2,1)}), bf16[192,3584]{1,0:T(8,128)(2,1)}) %reduce-scatter.18.cloned.1.call-update) | async-done | bytes 1376272 | tf_op jit(solution)/shard_map/reduce_scatter | solution.py:214
  717.6 4.8 copy.154
  722.5 4.6 reshape.246
  728.7 7.1 fusion.41
  735.8 40.6 %psum.7 = f32[5120]{0:T(1024)S(1)} all-reduce(f32[5120]{0:T(1024)S(1)} %pad_maximum_fusion.13), channel_id=1, replica_groups=mesh['dp'=8,'tensor'=4] {'dp','tensor'}, use_global_device_ids=true, to_apply=%region_13.14 | all-reduce | flops 5120 | bytes 40960 | tf_op jit(solution)/shard_map/psum | solution.py:223
  777.5 2.8 fusion.40
  780.4 2.7 reduce-scatter.26.cloned.1.call-done
  783.0 2.5 convert_element_type.165
  785.5 66.5 %reduce-scatter.22.cloned.1.call-done = bf16[192,2240]{1,0:T(8,128)(2,1)} async-done(((bf16[1536,2240]{1,0:T(8,128)(2,1)}), bf16[192,2240]{1,0:T(8,128)(2,1)}) %reduce-scatter.22.cloned.1.call-update) | async-done | bytes 860176 | tf_op jit(solution)/shard_map/reduce_scatter | solution.py:214
  852.1 2.5 convert_element_type.161
  854.6 66.4 %reduce-scatter.24.cloned.1.call-done = bf16[192,2240]{1,0:T(8,128)(2,1)} async-done(((bf16[1536,2240]{1,0:T(8,128)(2,1)}), bf16[192,2240]{1,0:T(8,128)(2,1)}) %reduce-scatter.24.cloned.1.call-update) | async-done | bytes 860176 | tf_op jit(solution)/shard_map/reduce_scatter | solution.py:214
  921.0 2.5 convert_element_type.163
  923.5 19.8 %reduce-scatter.20.cloned.1.call-done = bf16[48,512]{1,0:T(8,128)(2,1)} async-done(((bf16[192,512]{1,0:T(8,128)(2,1)}), bf16[48,512]{1,0:T(8,128)(2,1)}) %reduce-scatter.20.cloned.1.call-update) | async-done | bytes 49168 | tf_op jit(solution)/shard_map/reduce_scatter | solution.py:220
  944.7 28.4 %reduce-scatter.28.cloned.1.call-done = bf16[384,384]{1,0:T(8,128)(2,1)} async-done(((bf16[1536,384]{1,0:T(8,128)(2,1)}), bf16[384,384]{1,0:T(8,128)(2,1)}) %reduce-scatter.28.cloned.1.call-update) | async-done | bytes 294928
  (171 shorter events, 44.0 us)
Async XLA Ops:
  7.2 113.1 %copy-start = (s32[1,1024]{1,0:T(1,128)S(1)}, s32[1,1024]{1,0:T(1,128)}, u32[]{:S(2)}) copy-start(s32[1,1024]{1,0:T(1,128)} %param.16) | copy-start | bytes 12292
  7.2 39.5 %copy-start.28 = (bf16[192]{0:T(256)(128)(2,1)S(1)}, bf16[192]{0:T(256)(128)(2,1)}, u32[]{:S(2)}) copy-start(bf16[192]{0:T(256)(128)(2,1)} %param.17) | copy-start | bytes 1156
  7.2 39.5 %copy-start.29 = (bf16[192]{0:T(256)(128)(2,1)S(1)}, bf16[192]{0:T(256)(128)(2,1)}, u32[]{:S(2)}) copy-start(bf16[192]{0:T(256)(128)(2,1)} %param.25) | copy-start | bytes 1156
  7.2 48.5 %copy-start.24 = (bf16[384]{0:T(512)(128)(2,1)S(1)}, bf16[384]{0:T(512)(128)(2,1)}, u32[]{:S(2)}) copy-start(bf16[384]{0:T(512)(128)(2,1)} %param.19) | copy-start | bytes 2308
  7.2 61.6 %copy-start.26 = (bf16[256]{0:T(256)(128)(2,1)S(1)}, bf16[256]{0:T(256)(128)(2,1)}, u32[]{:S(2)}) copy-start(bf16[256]{0:T(256)(128)(2,1)} %param.21) | copy-start | bytes 1540
  7.2 61.6 %copy-start.25 = (bf16[256]{0:T(256)(128)(2,1)S(1)}, bf16[256]{0:T(256)(128)(2,1)}, u32[]{:S(2)}) copy-start(bf16[256]{0:T(256)(128)(2,1)} %param.23) | copy-start | bytes 1540
  7.2 61.7 %copy-start.4 = (bf16[256,1536]{1,0:T(8,128)(2,1)S(1)}, bf16[256,1536]{1,0:T(8,128)(2,1)}, u32[]{:S(2)}) copy-start(bf16[256,1536]{1,0:T(8,128)(2,1)} %param.15) | copy-start | bytes 2359300
  7.3 35.9 %all-gather.10.cloned.1.call-start = ((), (), s32[]{:S(2)}) async-start(), calls=%async_computation.9 | async-start | bytes 1474560 | tf_op jit(solution)/shard_map/all_gather | solution.py:96
  9.1 102.3 %all-gather.12.cloned.1.call-start = ((), (), s32[]{:S(2)}) async-start(), calls=%async_computation.10 | async-start | bytes 12386304 | tf_op jit(solution)/shard_map/all_gather | solution.py:98
  46.6 100.9 %all-gather.14.cloned.1.call-start = ((), (), s32[]{:S(2)}) async-start(), calls=%async_computation.11 | async-start | bytes 1310720 | tf_op jit(solution)/shard_map/all_gather | solution.py:124
  68.8 49.0 %copy-start.12 = (f32[256,64]{1,0:T(8,128)}, f32[256,64]{1,0:T(8,128)S(1)}, u32[]{:S(2)}) copy-start(f32[256,64]{1,0:T(8,128)S(1)} %copy.112) | copy-start | bytes 196612
  68.9 47.2 %copy-start.19 = (f32[1536]{0:T(1024)}, f32[1536]{0:T(1024)S(1)}, u32[]{:S(2)}) copy-start(f32[1536]{0:T(1024)S(1)} %get-tuple-element.19) | copy-start | bytes 18436
  69.2 46.9 %copy-start.22 = (f32[256]{0:T(256)}, f32[256]{0:T(256)S(1)}, u32[]{:S(2)}) copy-start(f32[256]{0:T(256)S(1)} %add_rsqrt_fusion.1) | copy-start | bytes 3076
  116.1 1.4 copy-start.9
  119.4 141.6 %all-gather.18.cloned.1.call-start = ((), (), s32[]{:S(2)}) async-start(), calls=%async_computation.13 | async-start | bytes 7962624 | tf_op jit(solution)/shard_map/all_gather | solution.py:105
  120.0 153.8 %all-gather.16.cloned.1.call-start = ((), (), s32[]{:S(2)}) async-start(), calls=%async_computation.12 | async-start | bytes 3932160 | tf_op jit(solution)/shard_map/all_gather | solution.py:151
  125.9 27.7 %copy-start.5 = (bf16[256,12,64]{2,0,1:T(8,128)(2,1)}, bf16[256,12,64]{2,0,1:T(8,128)(2,1)S(1)}, u32[]{:S(2)}) copy-start(bf16[256,12,64]{2,0,1:T(8,128)(2,1)S(1)} %copy.115) | copy-start | bytes 1179652
  126.3 27.3 %copy-start.6 = (bf16[256,12,64]{2,0,1:T(8,128)(2,1)}, bf16[256,12,64]{2,0,1:T(8,128)(2,1)S(1)}, u32[]{:S(2)}) copy-start(bf16[256,12,64]{2,0,1:T(8,128)(2,1)S(1)} %copy.116) | copy-start | bytes 1179652
  151.3 4.3 copy-start.10
  153.6 4.0 copy-start.2
  155.6 4.5 copy-start.17
  160.1 4.2 copy-start.14
  164.3 312.7 %copy-start.3 = (f32[256,1536]{1,0:T(8,128)}, f32[256,1536]{1,0:T(8,128)S(1)}, u32[]{:S(2)}) copy-start(f32[256,1536]{1,0:T(8,128)S(1)} %get-tuple-element.58) | copy-start | bytes 4718596
  165.6 158.6 %all-gather.20.cloned.1.call-start = ((), (), s32[]{:S(2)}) async-start(), calls=%async_computation.14 | async-start | bytes 7962624 | tf_op jit(solution)/shard_map/all_gather | solution.py:106
  166.2 208.6 %all-gather.22.cloned.1.call-start = ((), (), s32[]{:S(2)}) async-start(), calls=%async_computation.15 | async-start | bytes 7962624 | tf_op jit(solution)/shard_map/all_gather | solution.py:107
  166.9 310.0 %reduce-scatter.14.cloned.1.call-start = ((), (), s32[]{:S(2)}) async-start(), calls=%async_computation.17 | async-start | bytes 3932160 | tf_op jit(solution)/shard_map/reduce_scatter | solution.py:163
  167.0 20.7 %collective-permute-start = (bf16[256,1536]{1,0:T(8,128)(2,1)}, bf16[256,1536]{1,0:T(8,128)(2,1)}, u32[]{:S(2)}, u32[]{:S(2)}) collective-permute-start(bf16[256,1536]{1,0:T(8,128)(2,1)} %param.29), channel_id=1, source_target_pairs={{0,1},{1,2},{2,3},{3,0},{4,5},{5,6},{6,7},{7,4},{8,9},{9,10},{10,1... | collective-permute-start | bytes 2359304 | tf_op jit(solution)/shard_map/ppermute | solution.py:20
  187.6 22.5 %collective-permute-start.1 = (bf16[256,1536]{1,0:T(8,128)(2,1)}, bf16[256,1536]{1,0:T(8,128)(2,1)}, u32[]{:S(2)}, u32[]{:S(2)}) collective-permute-start(bf16[256,1536]{1,0:T(8,128)(2,1)} %collective-permute-done), channel_id=1, source_target_pairs={{0,1},{1,2},{2,3},{3,0},{4,5},{5,6},{6,7},{7,4},{8,9},{9,10},{10,1... | collective-permute-start | bytes 2359304 | tf_op jit(solution)/shard_map/ppermute | solution.py:20
  187.6 64.0 %collective-permute-start.2 = (bf16[256,1536]{1,0:T(8,128)(2,1)}, bf16[256,1536]{1,0:T(8,128)(2,1)}, u32[]{:S(2)}, u32[]{:S(2)}) collective-permute-start(bf16[256,1536]{1,0:T(8,128)(2,1)} %param.29), channel_id=1, source_target_pairs={{0,3},{1,0},{2,1},{3,2},{4,7},{5,4},{6,5},{7,6},{8,11},{9,8},{10,9... | collective-permute-start | bytes 2359304 | tf_op jit(solution)/shard_map/ppermute | solution.py:22
  192.0 65.9 %copy-start.7 = (bf16[256,1536]{1,0:T(8,128)(2,1)S(1)}, bf16[256,1536]{1,0:T(8,128)(2,1)}, u32[]{:S(2)}) copy-start(bf16[256,1536]{1,0:T(8,128)(2,1)} %param.29) | copy-start | bytes 2359300
  395.8 11.4 %copy-start.27 = (bf16[1536,2240]{1,0:T(8,128)(2,1)S(1)}, bf16[1536,2240]{1,0:T(8,128)(2,1)}, u32[]{:S(2)}) copy-start(bf16[1536,2240]{1,0:T(8,128)(2,1)} %all-gather.20.cloned.1.call-done) | copy-start | bytes 20643844
  395.8 11.4 %copy-start.30 = (bf16[1024,2240]{0,1:T(8,128)(2,1)S(1)}, bf16[1024,2240]{0,1:T(8,128)(2,1)}, u32[]{:S(2)}) copy-start(bf16[1024,2240]{0,1:T(8,128)(2,1)} %get-tuple-element.20) | copy-start | bytes 13762564
  416.5 123.1 %reduce-scatter.12.cloned.1.call-start = ((), (), s32[]{:S(2)}) async-start(), calls=%async_computation.16 | async-start | bytes 3932160 | tf_op jit(solution)/shard_map/reduce_scatter | solution.py:156
  429.0 189.7 %reduce-scatter.16.cloned.1.call-start = ((), (), s32[]{:S(2)}) async-start(), calls=%async_computation.18 | async-start | bytes 1310720 | tf_op jit(solution)/shard_map/reduce_scatter | solution.py:197
  543.1 7.0 copy-start.11
  543.1 7.0 copy-start.18
  550.1 9.2 copy-start.8
  576.7 14.8 %copy-start.16 = (f32[256,64]{0,1:T(8,128)S(1)}, f32[256,64]{0,1:T(8,128)}, u32[]{:S(2)}) copy-start(f32[256,64]{0,1:T(8,128)} %get-tuple-element.52) | copy-start | bytes 196612
  591.3 121.9 %reduce-scatter.18.cloned.1.call-start = ((), (), s32[]{:S(2)}) async-start(), calls=%async_computation.19 | async-start | bytes 12386304 | tf_op jit(solution)/shard_map/reduce_scatter | solution.py:214
  592.3 4.4 copy-start.15
  596.7 23.3 %copy-start.13 = (f32[256,64]{1,0:T(8,128)S(1)}, f32[256,64]{1,0:T(8,128)}, u32[]{:S(2)}) copy-start(f32[256,64]{1,0:T(8,128)} %copy-done.12) | copy-start | bytes 196612
  596.7 25.0 %copy-start.20 = (f32[1536]{0:T(1024)S(1)}, f32[1536]{0:T(1024)}, u32[]{:S(2)}) copy-start(f32[1536]{0:T(1024)} %copy-done.19) | copy-start | bytes 18436
  596.7 25.0 %copy-start.23 = (f32[256]{0:T(256)S(1)}, f32[256]{0:T(256)}, u32[]{:S(2)}) copy-start(f32[256]{0:T(256)} %copy-done.22) | copy-start | bytes 3076
  621.6 3.4 slice-start
  621.7 3.3 slice-start.1
  630.2 152.8 %reduce-scatter.26.cloned.1.call-start = ((), (), s32[]{:S(2)}) async-start(), calls=%async_computation.23 | async-start | bytes 7962624 | tf_op jit(solution)/shard_map/reduce_scatter | solution.py:214
  643.0 209.1 %reduce-scatter.22.cloned.1.call-start = ((), (), s32[]{:S(2)}) async-start(), calls=%async_computation.21 | async-start | bytes 7962624 | tf_op jit(solution)/shard_map/reduce_scatter | solution.py:214
  656.9 264.1 %reduce-scatter.24.cloned.1.call-start = ((), (), s32[]{:S(2)}) async-start(), calls=%async_computation.22 | async-start | bytes 7962624 | tf_op jit(solution)/shard_map/reduce_scatter | solution.py:214
  669.3 274.0 %reduce-scatter.20.cloned.1.call-start = ((), (), s32[]{:S(2)}) async-start(), calls=%async_computation.20 | async-start | bytes 245760 | tf_op jit(solution)/shard_map/reduce_scatter | solution.py:220
  714.9 258.2 %reduce-scatter.28.cloned.1.call-start = ((), (), s32[]{:S(2)}) async-start(), calls=%async_computation.24 | async-start | bytes 1474560
  728.7 7.1 copy-start.21
  783.0 192.9 %copy-start.1 = (s32[1,1024]{1,0:T(1,128)S(1)}, s32[1,1024]{1,0:T(1,128)}, u32[]{:S(2)}) copy-start(s32[1,1024]{1,0:T(1,128)} %param.16) | copy-start | bytes 12292
Sparse Core Ops, SparseCore 0:
  10.2 32.8 all-gather.9
  46.7 64.6 all-gather.11
  119.5 27.9 all-gather.13
  149.2 48.0 all-gather.17
  199.4 74.3 all-gather.15
  275.5 48.6 all-gather.19
  326.1 48.7 all-gather.21
  416.6 60.2 reduce-scatter.13
  479.2 60.3 reduce-scatter.11
  591.5 27.1 reduce-scatter.15
  630.3 82.8 reduce-scatter.17
  716.6 66.3 reduce-scatter.25
  786.5 65.4 reduce-scatter.21
  855.4 65.4 reduce-scatter.23
  923.7 19.5 reduce-scatter.19
  945.5 27.5 reduce-scatter.27
